TPU v7x, 32 devices: a whole 2x2x4 slice. The times are simulated.
32 devices in a mesh: replica: 16 (over z, x, core), spatial: 2 (over y).
Axes of the slice: x: 2, y: 2, z: 4, core: 2. Of those that a mesh axis runs over, the one named last changes fastest.
Arguments:
- grads: bfloat16 [16, 2, 852992], P('replica', 'spatial'), may hold values from -6 to 6
- master: float32 [852992], P(('replica', 'spatial')), may hold values from -0.06 to 0.06
- velocity: float32 [852992], P(('replica', 'spatial')), may hold values from -0.3 to 0.3
- layer_offsets: int32 [6], replicated, may hold values from 0 to 852736, as said below
- layer_sizes: int32 [6], replicated, may hold values from 256 to 589824
- lars_skip: int32 [6], replicated, may hold values from 0 to 1
Outputs:
- new_weights: bfloat16 [852992], replicated
- new_master: float32 [852992], P(('replica', 'spatial'))
- new_velocity: float32 [852992], P(('replica', 'spatial'))
Inputs may be any that keep to these rules, and one draw needn't show every extreme that they name: layer_offsets, layer_sizes and lars_skip describe the six tensors (a 256 x 1024 convolution, a 256 x 256 x 9 convolution, and two gains and two shifts of 256 entries) laid end to end in some order without gaps, the last of them always a gain or a shift; lars_skip is 1 exactly for the gains and shifts.
All inputs are finite; a program needn't handle non-finite values.
Results may differ from a plain program's by a relative error of at most 0.001.
Values may be sent and summed in bfloat16 or wider, within the bound.
A program may use at most 64 MiB of HBM per device.

v0:
```python
import jax
import jax.numpy as jnp
from jax import lax
from jax.sharding import PartitionSpec as P


def shards(grads, master, velocity, layer_offsets, layer_sizes, lars_skip):
    n_rep = lax.axis_size("replica")
    n_spa = lax.axis_size("spatial")
    shard = master.shape[0]
    position = lax.axis_index(("replica", "spatial")) * shard + jnp.arange(shard, dtype=jnp.int32)
    inside = (position[None, :] >= layer_offsets[:, None]) & (
        position[None, :] < (layer_offsets + layer_sizes)[:, None]
    )
    onehot = inside.astype(jnp.float32)
    received = lax.all_to_all(
        grads[0, 0].reshape(n_rep, n_spa * shard),
        "replica",
        split_axis=0,
        concat_axis=0,
        tiled=True,
    )
    first = jnp.sum(received.astype(jnp.float32), axis=0)
    summed = lax.psum_scatter(
        first.reshape(n_spa, shard), "spatial", scatter_dimension=0, tiled=True
    )
    grad = summed.reshape(shard) / (n_rep * n_spa)
    gsq_local = jnp.dot(onehot, grad * grad, precision=lax.Precision.HIGHEST)
    wsq_local = jnp.dot(onehot, master * master, precision=lax.Precision.HIGHEST)
    wsq, gsq = lax.psum((wsq_local, gsq_local), ("replica", "spatial"))
    wnorm = jnp.sqrt(wsq)
    gnorm = jnp.sqrt(gsq)
    skipped = lars_skip.astype(jnp.float32)
    ratio = 0.02 * wnorm / (gnorm + 0.001 * wnorm + 1e-06)
    trust = skipped + (1.0 - skipped) * ratio
    decay = (1.0 - skipped) * 0.001
    trust_pos = jnp.dot(trust, onehot, precision=lax.Precision.HIGHEST)
    decay_pos = jnp.dot(decay, onehot, precision=lax.Precision.HIGHEST)
    new_velocity = 0.9 * velocity + 8.0 * trust_pos * (grad + decay_pos * master)
    new_master = master - new_velocity
    new_weights = lax.all_gather(
        new_master.astype(jnp.bfloat16), ("replica", "spatial"), axis=0, tiled=True
    )
    return (new_weights, new_master, new_velocity)


def solution(mesh):
    return jax.shard_map(
        shards,
        mesh=mesh,
        in_specs=(
            P("replica", "spatial", None),
            P(("replica", "spatial")),
            P(("replica", "spatial")),
            P(),
            P(),
            P(),
        ),
        out_specs=(P(), P(("replica", "spatial")), P(("replica", "spatial"))),
        check_vma=False,
    )
```

profile of v0, /device:TPU:0, one launch (start us, length us, event | category | flops | bytes accessed | tf_op | source)
XLA Modules:
  0.0 341.0 jit_solution(4959349934665128111)
XLA Ops:
  7.2 37.8 %reduce.1 = bf16[852992]{0:T(1024)(128)(2,1)} reduce(bf16[1,1,852992]{2,1,0:T(2,128)(2,1)} %param.6, bf16[]{:T(256)} %constant.38), dimensions={0,1}, to_apply=%param.6.reduce_sub_computation | reduce | bytes 3411970 | tf_op args[0]
  44.9 3.0 all_to_all.8
  47.9 0.5 broadcast.54
  48.4 13.3 %reduce.8 = bf16[16,53312]{1,0:T(8,128)(2,1)} reduce(bf16[16,1,53312]{2,1,0:T(2,128)(2,1)S(1)} %all_to_all.8, bf16[]{:T(256)} %broadcast.54), dimensions={1}, to_apply=%all_to_all.8.reduce_sub_computation | reduce | bytes 3411970 | tf_op jit(solution)/shard_map/all_to_all | solution.py:16
  61.8 3.2 reshape.38
  65.0 0.0 copy-start.1
  65.0 0.0 copy-start.4
  65.0 0.0 copy-start.6
  65.0 0.0 copy-start.7
  65.0 7.6 %all-to-all-start = ((bf16[16,2,26656]{2,1,0:T(2,128)(2,1)}), bf16[16,2,26656]{2,1,0:T(2,128)(2,1)}, u32[]{:S(2)}, u32[]{:S(2)}) async-start(bf16[16,2,26656]{2,1,0:T(2,128)(2,1)} %reshape.38), calls=%async_computation | async-start | bytes 3424256 | tf_op jit(solution)/shard_map/all_to_all | solution.py:16
  72.5 0.0 all-reduce.8.cloned.1.call-start
  72.6 0.0 copy-done.1
  72.6 0.7 reshape.25
  73.4 0.0 copy-done.4
  73.4 0.0 copy-done.6
  73.4 0.0 copy-done.7
  73.4 0.7 dynamic-slice
  74.1 0.7 iota_add_fusion
  74.7 32.2 %all-to-all-done = bf16[16,2,26656]{2,1,0:T(2,128)(2,1)} async-done(((bf16[16,2,26656]{2,1,0:T(2,128)(2,1)}), bf16[16,2,26656]{2,1,0:T(2,128)(2,1)}, u32[]{:S(2)}, u32[]{:S(2)}) %all-to-all-start) | async-done | bytes 1706016 | tf_op jit(solution)/shard_map/all_to_all | solution.py:16
  106.9 10.5 %reshape.39 = bf16[16,1,53312]{2,1,0:T(2,128)(2,1)S(1)} reshape(bf16[16,2,26656]{2,1,0:T(2,128)(2,1)} %all-to-all-done) | data formatting | bytes 3411968
  117.4 0.0 copy-start.5
  117.4 5.2 %convert_reduce_fusion = f32[53312]{0:T(1024)} fusion(bf16[16,1,53312]{2,1,0:T(2,128)(2,1)S(1)} %reshape.39), kind=kLoop, calls=%fused_computation | loop fusion | flops 1652672 | bytes 1919232 | tf_op jit(solution)/shard_map/reduce_sum | solution.py:23
  122.6 0.0 copy-start.3
  122.6 1.8 reshape.22
  124.5 0.0 all-reduce.8.cloned.1.call-update
  124.5 0.0 all-reduce.6.cloned.1.call-start
  124.5 0.0 copy-done.5
  124.5 1.7 convolution_reduce_fusion
  126.2 0.0 copy-start.2
  126.3 2.1 convolution_bitcast_fusion.1
  128.3 24.0 %all-reduce.8.cloned.1.call-done = f32[2,26656]{1,0:T(2,128)} async-done(((f32[2,26656]{1,0:T(2,128)}), f32[2,26656]{1,0:T(2,128)}) %all-reduce.8.cloned.1.call-update) | async-done | bytes 213264
  152.3 2.0 fusion
  154.3 0.1 reshape.27
  154.4 0.0 copy-done.3
  154.4 1.1 convolution_bitcast_fusion
  155.5 39.4 %all-reduce.2 = (f32[6]{0:T(128)S(1)}, f32[6]{0:T(128)S(1)}) all-reduce(f32[6]{0:T(128)S(1)} %convolution_bitcast_fusion, f32[6]{0:T(128)S(1)} %convolution_bitcast_fusion.1), channel_id=1, replica_groups=mesh['replica'=16,'spatial'=2] {'replica','spatial'}, use_global_device_ids=true, to_apply=%region_3.0 | all-reduce | flops 12 | bytes 96 | tf_op jit(solution)/shard_map/psum | solution.py:30
  194.9 0.8 convolution_reduce_fusion.1
  195.8 0.0 copy-done.2
  195.8 0.7 fusion.22
  196.5 0.1 broadcast.25
  196.6 0.6 dynamic-update-slice
  197.2 0.0 copy-start
  197.2 1.2 copy-done
  198.4 0.0 all-reduce.6.cloned.1.call-update
  198.4 133.0 %all-reduce.6.cloned.1.call-done = bf16[852992]{0:T(1024)(128)(2,1)} async-done(((bf16[852992]{0:T(1024)(128)(2,1)}), bf16[852992]{0:T(1024)(128)(2,1)}) %all-reduce.6.cloned.1.call-update) | async-done | bytes 1706000
  331.5 2.7 copy.13
  (3 shorter events, 0.0 us)
Async XLA Ops:
  65.0 7.7 %copy-start.1 = (f32[26656]{0:T(1024)S(1)}, f32[26656]{0:T(1024)}, u32[]{:S(2)}) copy-start(f32[26656]{0:T(1024)} %param.7) | copy-start | bytes 319876
  65.0 8.4 %copy-start.4 = (s32[6]{0:T(128)S(1)}, s32[6]{0:T(128)}, u32[]{:S(2)}) copy-start(s32[6]{0:T(128)} %param.10) | copy-start | bytes 76
  65.0 8.4 %copy-start.6 = (s32[6]{0:T(128)S(1)}, s32[6]{0:T(128)}, u32[]{:S(2)}) copy-start(s32[6]{0:T(128)} %param.9) | copy-start | bytes 76
  65.0 8.4 %copy-start.7 = (u32[32]{0:T(128)S(1)}, u32[32]{0:T(128)}, u32[]{:S(2)}) copy-start(u32[32]{0:T(128)} %constant.36) | copy-start | bytes 388
  65.0 41.9 %all-to-all-start = ((bf16[16,2,26656]{2,1,0:T(2,128)(2,1)}), bf16[16,2,26656]{2,1,0:T(2,128)(2,1)}, u32[]{:S(2)}, u32[]{:S(2)}) async-start(bf16[16,2,26656]{2,1,0:T(2,128)(2,1)} %reshape.38), calls=%async_computation | async-start | bytes 3424256 | tf_op jit(solution)/shard_map/all_to_all | solution.py:16
  72.5 79.8 %all-reduce.8.cloned.1.call-start = ((), (), s32[]{:S(2)}) async-start(), calls=%async_computation.2 | async-start | bytes 428032
  117.4 7.1 %copy-start.5 = (s32[6]{0:T(128)S(1)}, s32[6]{0:T(128)}, u32[]{:S(2)}) copy-start(s32[6]{0:T(128)} %param.11) | copy-start | bytes 76
  122.6 31.8 %copy-start.3 = (s32[26656]{0:T(1024)S(1)}, s32[26656]{0:T(1024)}, u32[]{:S(2)}) copy-start(s32[26656]{0:T(1024)} %iota_add_fusion) | copy-start | bytes 319876
  124.5 207.0 %all-reduce.6.cloned.1.call-start = ((), (), s32[]{:S(2)}) async-start(), calls=%async_computation.1 | async-start | bytes 3411968
  126.2 69.5 %copy-start.2 = (f32[26656]{0:T(1024)S(1)}, f32[26656]{0:T(1024)}, u32[]{:S(2)}) copy-start(f32[26656]{0:T(1024)} %param.8) | copy-start | bytes 319876
  197.2 1.2 copy-start
Sparse Core Ops, SparseCore 0:
  124.6 27.6 all-reduce.7
  198.6 132.8 all-reduce.5
where the time goes:
time: 342 us; the launch traced here: 341 us
  waiting for transfers between devices  189 us (55%)
  other arithmetic  59.7 us (17%)
  blocking collectives  39.4 us (12%)
  local copies, waits for them, and re-layouts  25.2 us (7%)
  between operations  14.2 us (4%)
  starting transfers between devices  7.66 us (2%)
  matrix products  5.68 us (2%)
    unnamed x4, waiting for transfers between devices  157 us
    psum x1, blocking collectives, shards(): wsq, gsq = lax.psum((wsq_local, gsq_local), ('replica', 'spatial'))  39.4 us
    unnamed x1, other arithmetic  37.8 us
    all_to_all x1, waiting for transfers between devices, shards(): lax.all_to_all(grads[0, 0].reshape(n_rep, n_spa * shard), 'replica', spli...  32.2 us
    unnamed x22, local copies, waits for them, and re-layouts  19.1 us
    all_to_all x1, other arithmetic, shards(): lax.all_to_all(grads[0, 0].reshape(n_rep, n_spa * shard), 'replica', spli...  13.3 us
    all_to_all x1, starting transfers between devices, shards(): lax.all_to_all(grads[0, 0].reshape(n_rep, n_spa * shard), 'replica', spli...  7.57 us
  transfers between devices with their start and end apart: 3, of which 3 were waited for; matrix products, arithmetic and copies ran while one was open for 2% of the time, Pallas kernels for 0%

commit v1 on v0

--- a/solution.py
+++ b/solution.py
@@ -1,7 +1,458 @@
+import functools
+import math
+
 import jax
 import jax.numpy as jnp
 from jax import lax
+from jax.experimental import pallas as pl
+from jax.experimental.pallas import tpu as pltpu
 from jax.sharding import PartitionSpec as P
+
+MESH = pl.DeviceIdType.MESH
+TILE = 1024
+
+
+def kernel(
+    plan,
+    grads_ref,
+    m_ref,
+    v_ref,
+    offsets_ref,
+    sizes_ref,
+    skip_ref,
+    out_ref,
+    nm_ref,
+    nv_ref,
+    gin,
+    packed,
+    recv1,
+    part,
+    recv2,
+    mv,
+    halo,
+    grad_buf,
+    wrow,
+    stats,
+    ags,
+    nmw,
+    nvw,
+    in_sem,
+    send1,
+    got1,
+    send2,
+    got2,
+    halo_sem,
+    send3,
+    got3,
+    send4,
+    got4,
+    out_sem,
+):
+    n_out, n_a, n_spa, shard, step, span, layers = plan
+    plane = n_a * 2 * n_spa
+    n = n_out * plane
+    chunk = (plane - 1) * step + span
+    rows = span * 8
+    r = lax.axis_index("replica")
+    s = lax.axis_index("spatial")
+    d = r * n_spa + s
+    z = d // plane
+    p = d % plane
+    a = p // (2 * n_spa)
+    c = (p // n_spa) % 2
+    base = d * (step * TILE)
+    off = d * (shard - step * TILE)
+
+    def dev(flat):
+        return (flat // n_spa, flat % n_spa)
+
+    barrier = pltpu.get_barrier_semaphore()
+
+    @pl.loop(1, n)
+    def _(q):
+        pl.semaphore_signal(barrier, inc=1, device_id=dev((d + q) % n), device_id_type=MESH)
+
+    def load(zt):
+        start = pl.multiple_of(zt * (plane * step * TILE), TILE)
+        return pltpu.make_async_copy(
+            grads_ref.at[0, :, pl.ds(start, chunk * TILE)], gin.at[zt], in_sem.at[zt]
+        )
+
+    for k in range(1, n_out + 1):
+        load((z + k) % n_out).start()
+
+    group = max(g for g in range(1, 33) if chunk % g == 0)
+
+    def pack(zt):
+        load(zt).wait()
+
+        @pl.loop(0, chunk // group)
+        def _(i):
+            at = pl.multiple_of(i * (group * TILE), group * TILE)
+            v = gin[zt, :, pl.ds(at, group * TILE)].astype(jnp.float32)
+            packed[zt, pl.ds(i * group, group)] = v.reshape(group, 8, 128).astype(jnp.bfloat16)
+
+    def copy1(zt, src, dst):
+        return pltpu.make_async_remote_copy(
+            src_ref=packed.at[zt, pl.ds(dst * step, span)],
+            dst_ref=recv1.at[zt, src],
+            send_sem=send1.at[zt, dst],
+            recv_sem=got1.at[zt, src],
+            device_id=dev(z * plane + dst),
+            device_id_type=MESH,
+        )
+
+    for k in range(1, n_out + 1):
+        zt = (z + k) % n_out
+        pack(zt)
+        if k == 1:
+            pl.semaphore_wait(barrier, n - 1)
+
+        @pl.loop(1, plane)
+        def _(q):
+            copy1(zt, p, (p + q) % plane).start()
+
+    lane = lax.broadcasted_iota(jnp.int32, (rows, 128), 1)
+    shift_l = off % 128
+    shift_r = off // 128
+    for j, ref in enumerate((m_ref, v_ref)):
+        x = pltpu.roll(ref[...], shift_l, 1)
+        x = jnp.where(lane < shift_l, pltpu.roll(x, 1, 0), x)
+        x = pltpu.roll(x, shift_r, 0)
+        mv[:, j] = x.reshape(span, 8, 128)
+    halo_copy = pltpu.make_async_remote_copy(
+        src_ref=mv.at[span - 1],
+        dst_ref=halo,
+        send_sem=halo_sem.at[0],
+        recv_sem=halo_sem.at[1],
+        device_id=dev((d + 1) % n),
+        device_id_type=MESH,
+    )
+    halo_copy.start()
+
+    place = lax.broadcasted_iota(jnp.int32, (8, 128), 0) * 128 + lax.broadcasted_iota(
+        jnp.int32, (8, 128), 1
+    )
+    low = [offsets_ref[l] - base for l in range(layers)]
+    high = [offsets_ref[l] + sizes_ref[l] - base for l in range(layers)]
+    own_low = [jnp.maximum(x, off) for x in low]
+    own_high = [jnp.minimum(x, off + shard) for x in high]
+    lane1 = lax.broadcasted_iota(jnp.int32, (1, 128), 1)
+
+    def squares(value, first):
+        def add(t, accs):
+            pos = place + t * TILE
+            x = value(t)
+            x = x * x
+            return tuple(
+                acc + jnp.where((pos >= lo) & (pos < hi), x, 0.0)
+                for acc, lo, hi in zip(accs, own_low, own_high)
+            )
+
+        accs = lax.fori_loop(
+            0, span, add, tuple(jnp.zeros((8, 128), jnp.float32) for _ in range(layers))
+        )
+        row = jnp.zeros((1, 128), jnp.float32)
+        for l, acc in enumerate(accs):
+            row = jnp.where(lane1 == first + l, jnp.sum(acc, axis=(0, 1), keepdims=True), row)
+        return row
+
+    wrow[...] = squares(lambda t: mv[t, 0], 0)
+
+    def copy2(zt, src):
+        return pltpu.make_async_remote_copy(
+            src_ref=part.at[zt],
+            dst_ref=recv2.at[src],
+            send_sem=send2.at[zt],
+            recv_sem=got2.at[src],
+            device_id=dev(zt * plane + p),
+            device_id_type=MESH,
+        )
+
+    for k in range(1, n_out + 1):
+        zt = (z + k) % n_out
+
+        @pl.loop(1, plane)
+        def _(q):
+            copy1(zt, (p + q) % plane, p).wait_recv()
+
+        @pl.loop(0, span)
+        def _(t):
+            acc = packed[zt, p * step + t].astype(jnp.float32)
+            for q in range(1, plane):
+                acc = acc + recv1[zt, (p + q) % plane, t].astype(jnp.float32)
+            part[zt, t] = acc
+
+        if k < n_out:
+            copy2(zt, z).start()
+
+    halo_copy.wait()
+    for j in range(2):
+        mv[0, j] = jnp.where(place < off, halo[j], mv[0, j])
+
+    @pl.loop(1, n_out)
+    def _(k):
+        copy2(z, (z + k) % n_out).wait_recv()
+
+    @pl.loop(0, span)
+    def _(t):
+        acc = part[z, t]
+        for k in range(1, n_out):
+            acc = acc + recv2[(z + k) % n_out, t]
+        grad_buf[t] = acc / n
+
+    stats[d] = squares(lambda t: grad_buf[t], layers) + wrow[...]
+
+    def copy3(src, dst):
+        return pltpu.make_async_remote_copy(
+            src_ref=stats.at[src],
+            dst_ref=stats.at[src],
+            send_sem=send3.at[dst],
+            recv_sem=got3.at[src],
+            device_id=dev(dst),
+            device_id_type=MESH,
+        )
+
+    @pl.loop(1, n)
+    def _(q):
+        copy3(d, (d + q) % n).start()
+
+    @pl.loop(1, n)
+    def _(q):
+        copy3((d + q) % n, d).wait_recv()
+
+    total = jnp.sum(stats[...], axis=0)
+    trust, decay = [], []
+    for l in range(layers):
+        wsq = jnp.sum(jnp.where(lane1 == l, total, 0.0), axis=(0, 1), keepdims=True)
+        gsq = jnp.sum(jnp.where(lane1 == layers + l, total, 0.0), axis=(0, 1), keepdims=True)
+        wnorm = jnp.sqrt(jnp.broadcast_to(wsq, (8, 128)))
+        gnorm = jnp.sqrt(jnp.broadcast_to(gsq, (8, 128)))
+        skipped = skip_ref[l].astype(jnp.float32)
+        ratio = 0.02 * wnorm / (gnorm + 0.001 * wnorm + 1e-06)
+        trust.append(skipped + (1.0 - skipped) * ratio)
+        decay.append((1.0 - skipped) * 0.001)
+
+    @pl.loop(0, span)
+    def _(t):
+        pos = place + t * TILE
+        trust_pos = jnp.zeros((8, 128), jnp.float32)
+        decay_pos = jnp.zeros((8, 128), jnp.float32)
+        for l in range(layers):
+            inside = (pos >= low[l]) & (pos < high[l])
+            trust_pos = jnp.where(inside, trust[l], trust_pos)
+            decay_pos = jnp.where(inside, decay[l], decay_pos)
+        m = mv[t, 0]
+        nv = 0.9 * mv[t, 1] + 8.0 * trust_pos * (grad_buf[t] + decay_pos * m)
+        nm = m - nv
+        nvw[t] = nv
+        nmw[t] = nm
+        ags[d, t] = nm.astype(jnp.bfloat16)
+
+    def copy4(block, slot, dst):
+        return pltpu.make_async_remote_copy(
+            src_ref=ags.at[block],
+            dst_ref=ags.at[block],
+            send_sem=send4.at[slot],
+            recv_sem=got4.at[block],
+            device_id=dev(dst),
+            device_id_type=MESH,
+        )
+
+    n_same = plane // 2
+    me_same = a * n_spa + s
+    partner = z * plane + a * (2 * n_spa) + (1 - c) * n_spa + s
+
+    def same(index, core):
+        return (index // n_spa) * (2 * n_spa) + core * n_spa + index % n_spa
+
+    def put(block):
+        return pltpu.make_async_copy(
+            ags.at[block, pl.ds(0, step)], out_ref.at[pl.ds(block * step, step)], out_sem.at[block]
+        )
+
+    def to_plane(zz):
+        block = zz * plane + p
+
+        @pl.loop(1, n_same)
+        def _(q):
+            peer = (me_same + q) % n_same
+            copy4(block, n_out + zz * n_same + peer, z * plane + same(peer, c)).start()
+
+    def to_partner(zz, index):
+        block = zz * plane + same(index, c)
+        copy4(block, n_out + n_out * n_same + zz * n_same + index, partner).start()
+        put(block).start()
+
+    @pl.loop(1, n_out)
+    def _(k):
+        zz = (z + k) % n_out
+        copy4(d, zz, zz * plane + p).start()
+
+    to_plane(z)
+    to_partner(z, me_same)
+
+    back_l = 128 - shift_l
+    for ref, src in ((nm_ref, nmw), (nv_ref, nvw)):
+        x = src[...].reshape(rows, 128)
+        x = pltpu.roll(x, (rows - shift_r) % rows, 0)
+        x = pltpu.roll(x, back_l % 128, 1)
+        ref[...] = jnp.where(lane < back_l, x, pltpu.roll(x, rows - 1, 0))
+
+    @pl.loop(1, n_out)
+    def _(k):
+        zz = (z + k) % n_out
+        copy4(zz * plane + p, zz, d).wait_recv()
+        to_plane(zz)
+        to_partner(zz, me_same)
+
+    @pl.loop(0, n_out)
+    def _(k):
+        zz = (z + k) % n_out
+
+        @pl.loop(1, n_same)
+        def _(q):
+            peer = (me_same + q) % n_same
+            copy4(zz * plane + same(peer, c), 0, d).wait_recv()
+            to_partner(zz, peer)
+
+    @pl.loop(0, n_out)
+    def _(k):
+        zz = (z + k) % n_out
+
+        @pl.loop(0, n_same)
+        def _(q):
+            peer = (me_same + q) % n_same
+            block = zz * plane + same(peer, 1 - c)
+            copy4(block, 0, d).wait_recv()
+            put(block).start()
+
+    tail = pltpu.make_async_copy(
+        ags.at[n - 1, pl.ds(step, span - step)],
+        out_ref.at[pl.ds(n * step, span - step)],
+        out_sem.at[n],
+    )
+    tail.start()
+
+    @pl.loop(1, n_out)
+    def _(k):
+        zz = (z + k) % n_out
+        copy2(zz, z).wait_send()
+        copy4(d, zz, zz * plane + p).wait_send()
+
+    @pl.loop(0, n_out)
+    def _(zz):
+        @pl.loop(1, plane)
+        def _(q):
+            copy1(zz, p, (p + q) % plane).wait_send()
+
+        @pl.loop(1, n_same)
+        def _(q):
+            peer = (me_same + q) % n_same
+            copy4(zz * plane + p, n_out + zz * n_same + peer, z * plane + same(peer, c)).wait_send()
+
+        @pl.loop(0, n_same)
+        def _(index):
+            slot = n_out + n_out * n_same + zz * n_same + index
+            copy4(zz * plane + same(index, c), slot, partner).wait_send()
+
+    @pl.loop(1, n)
+    def _(q):
+        copy3(d, (d + q) % n).wait_send()
+
+    @pl.loop(0, n)
+    def _(block):
+        put(block).wait()
+
+    tail.wait()
+
+
+def windowed(n_rep, n_spa, grads, master, velocity, layer_offsets, layer_sizes, lars_skip):
+    shard = master.shape[0]
+    params = grads.shape[2]
+    layers = layer_offsets.shape[0]
+    n_in = math.isqrt(n_rep)
+    n_out, n_a = n_rep // n_in, n_in // 2
+    n = n_rep * n_spa
+    plane = n_in * n_spa
+    step = shard // TILE
+    span = params // TILE - (n - 1) * step
+    chunk = (plane - 1) * step + span
+    tiles = params // TILE
+    rows = span * 8
+    pad = span * TILE - shard
+    plan = (n_out, n_a, n_spa, shard, step, span, layers)
+    vmem = pl.BlockSpec(memory_space=pltpu.VMEM)
+    smem = pl.BlockSpec(memory_space=pltpu.SMEM)
+    anywhere = pl.BlockSpec(memory_space=pl.ANY)
+    f32, bf16 = jnp.float32, jnp.bfloat16
+    dma = pltpu.SemaphoreType.DMA
+    n_same = plane // 2
+    weights, nm, nv = pl.pallas_call(
+        functools.partial(kernel, plan),
+        out_shape=(
+            jax.ShapeDtypeStruct((tiles, 8, 128), bf16),
+            jax.ShapeDtypeStruct((rows, 128), f32),
+            jax.ShapeDtypeStruct((rows, 128), f32),
+        ),
+        in_specs=[anywhere, vmem, vmem, smem, smem, smem],
+        out_specs=(anywhere, vmem, vmem),
+        scratch_shapes=[
+            pltpu.VMEM((n_out, 1, chunk * TILE), bf16),
+            pltpu.VMEM((n_out, chunk, 8, 128), bf16),
+            pltpu.VMEM((n_out, plane, span, 8, 128), bf16),
+            pltpu.VMEM((n_out, span, 8, 128), f32),
+            pltpu.VMEM((n_out, span, 8, 128), f32),
+            pltpu.VMEM((span, 2, 8, 128), f32),
+            pltpu.VMEM((2, 8, 128), f32),
+            pltpu.VMEM((span, 8, 128), f32),
+            pltpu.VMEM((1, 128), f32),
+            pltpu.VMEM((n, 1, 128), f32),
+            pltpu.VMEM((n, span, 8, 128), bf16),
+            pltpu.VMEM((span, 8, 128), f32),
+            pltpu.VMEM((span, 8, 128), f32),
+            dma((n_out,)),
+            dma((n_out, plane)),
+            dma((n_out, plane)),
+            dma((n_out,)),
+            dma((n_out,)),
+            dma((2,)),
+            dma((n,)),
+            dma((n,)),
+            dma((n_out + 2 * n_out * n_same,)),
+            dma((n,)),
+            dma((n + 1,)),
+        ],
+        compiler_params=pltpu.CompilerParams(collective_id=0, has_side_effects=True),
+    )(
+        grads,
+        jnp.pad(master, (0, pad)).reshape(rows, 128),
+        jnp.pad(velocity, (0, pad)).reshape(rows, 128),
+        layer_offsets,
+        layer_sizes,
+        lars_skip,
+    )
+    return weights.reshape(params), nm.reshape(-1)[:shard], nv.reshape(-1)[:shard]
+
+
+def tiled(n_rep, n_spa, params):
+    n = n_rep * n_spa
+    shard = params // n
+    n_in = math.isqrt(n_rep)
+    rest = shard % TILE
+    return (
+        n_in * n_in == n_rep
+        and n_in % 2 == 0
+        and params % TILE == 0
+        and shard >= TILE
+        and 0 < n * rest <= TILE
+    )
+
+
+def step_fn(n_rep, n_spa, grads, *rest):
+    if tiled(n_rep, n_spa, grads.shape[2]):
+        return windowed(n_rep, n_spa, grads, *rest)
+    return shards(grads, *rest)
 
 
 def shards(grads, master, velocity, layer_offsets, layer_sizes, lars_skip):
@@ -46,7 +497,7 @@
 
 def solution(mesh):
     return jax.shard_map(
-        shards,
+        functools.partial(step_fn, mesh.shape["replica"], mesh.shape["spatial"]),
         mesh=mesh,
         in_specs=(
             P("replica", "spatial", None),

time: 342 us -> 60.9 us (0.18)
  waiting for transfers between devices: 189 us -> 0 us
  other arithmetic: 59.7 us -> 0 us
  Pallas kernels: 0 us -> 53.3 us
  blocking collectives: 39.4 us -> 0 us
  local copies, waits for them, and re-layouts: 25.2 us -> 5.75 us
  between operations: 14.2 us -> 0.66 us
  starting transfers between devices: 7.66 us -> 0 us
  matrix products: 5.68 us -> 0 us
    unnamed x4 -> x0, waiting for transfers between devices: 157 us -> none
    pallas_call x0 -> x1, Pallas kernels: none -> 53.3 us  [windowed(): pl.pallas_call(functools.partial(kernel, plan), out_shape=(jax.ShapeDtype...]
    psum x1 -> x0, blocking collectives: 39.4 us -> none  [shards(): wsq, gsq = lax.psum((wsq_local, gsq_local), ('replica', 'spatial'))]
    unnamed x1 -> x0, other arithmetic: 37.8 us -> none
    all_to_all x1 -> x0, waiting for transfers between devices: 32.2 us -> none  [shards(): lax.all_to_all(grads[0, 0].reshape(n_rep, n_spa * shard), 'replica', spli...]
    unnamed x22 -> x7, local copies, waits for them, and re-layouts: 19.1 us -> 4.1 us
    all_to_all x1 -> x0, other arithmetic: 13.3 us -> none  [shards(): lax.all_to_all(grads[0, 0].reshape(n_rep, n_spa * shard), 'replica', spli...]
    all_to_all x1 -> x0, starting transfers between devices: 7.57 us -> none  [shards(): lax.all_to_all(grads[0, 0].reshape(n_rep, n_spa * shard), 'replica', spli...]
  transfers between devices with their start and end apart: 3 -> 0, of which waited for: 3 -> 0; matrix products, arithmetic and copies ran while one was open for 2% -> 0% of each run, Pallas kernels for 0% -> 0%
where the time goes in v1:
time: 60.9 us; the launch traced here: 59.7 us
  Pallas kernels  53.3 us (88%)
  local copies, waits for them, and re-layouts  5.75 us (9%)
  between operations  0.66 us (1%)
    pallas_call x1, Pallas kernels, windowed(): pl.pallas_call(functools.partial(kernel, plan), out_shape=(jax.ShapeDtype...  53.3 us
    unnamed x7, local copies, waits for them, and re-layouts  4.1 us
    reshape x1, local copies, waits for them, and re-layouts, windowed(): jnp.pad(velocity, (0, pad)).reshape(rows, 128)  1.65 us

profile of v1, /device:TPU:0, one launch (start us, length us, event | category | flops | bytes accessed | tf_op | source)
XLA Modules:
  0.0 59.7 jit_solution(17752740262753586596)
XLA Ops:
  0.6 1.6 %pad_bitcast_fusion = (f32[216,128]{1,0:T(8,128)}, f32[216,128]{1,0:T(8,128)}) fusion(f32[26656]{0:T(1024)} %param.8, f32[26656]{0:T(1024)} %param.7), kind=kLoop, calls=%fused_computation | loop fusion | bytes 434432 | tf_op jit(solution)/shard_map/reshape | solution.py:430
  2.3 53.3 %shard_map.85 = (bf16[833,8,128]{2,1,0:T(8,128)(2,1)}, f32[216,128]{1,0:T(8,128)}, f32[216,128]{1,0:T(8,128)}) custom-call(bf16[1,1,852992]{2,1,0:T(2,128)(2,1)} %grads_ref.1, f32[216,128]{1,0:T(8,128)} %get-tuple-element.10.m_ref, f32[216,128]{1,0:T(8,128)} %get-tuple-element.9.v_ref, s32[6]{0:T(128)} %offsets_ref.1, s32[6]{0:T(128)} %sizes_ref.1, s32[6]{0:T(128)} %skip_ref.1), custom_call_target="tpu_custom_call" | custom-call | tf_op jit(solution)/shard_map/pallas_call | solution.py:391
  55.6 0.0 copy-start.1
  55.6 0.0 copy-start
  55.6 2.8 %copy.12 = bf16[852992]{0:T(1024)(128)(2,1)} copy(bf16[852992]{0:T(1024)(128)(2,1)} %bitcast.9) | data formatting | bytes 3411968
  58.4 0.0 copy-done.1
  58.4 0.7 %copy.13 = f32[26656]{0:T(1024)} copy(f32[26656]{0:T(1024)S(1)} %bitcast.11) | data formatting | bytes 213248
  59.1 0.0 copy-done
  59.1 0.7 %copy.14 = f32[26656]{0:T(1024)} copy(f32[26656]{0:T(1024)S(1)} %bitcast.10) | data formatting | bytes 213248
Async XLA Ops:
  55.6 2.8 %copy-start.1 = (f32[216,128]{1,0:T(8,128)S(1)}, f32[216,128]{1,0:T(8,128)}, u32[]{:S(2)}) copy-start(f32[216,128]{1,0:T(8,128)} %get-tuple-element.7) | copy-start | bytes 331780
  55.6 3.5 %copy-start = (f32[216,128]{1,0:T(8,128)S(1)}, f32[216,128]{1,0:T(8,128)}, u32[]{:S(2)}) copy-start(f32[216,128]{1,0:T(8,128)} %get-tuple-element.8) | copy-start | bytes 331780

commit v2 on v1

--- a/solution.py
+++ b/solution.py
@@ -20,9 +20,11 @@
     offsets_ref,
     sizes_ref,
     skip_ref,
-    out_ref,
-    nm_ref,
-    nv_ref,
+    ags,
+    nmw,
+    nvw,
+    m_in,
+    v_in,
     gin,
     packed,
     recv1,
@@ -33,10 +35,8 @@
     grad_buf,
     wrow,
     stats,
-    ags,
-    nmw,
-    nvw,
     in_sem,
+    mv_sem,
     send1,
     got1,
     send2,
@@ -46,7 +46,6 @@
     got3,
     send4,
     got4,
-    out_sem,
 ):
     n_out, n_a, n_spa, shard, step, span, layers = plan
     plane = n_a * 2 * n_spa
@@ -80,6 +79,12 @@
 
     for k in range(1, n_out + 1):
         load((z + k) % n_out).start()
+    mv_loads = [
+        pltpu.make_async_copy(ref, buf, mv_sem.at[j])
+        for j, (ref, buf) in enumerate(((m_ref, m_in), (v_ref, v_in)))
+    ]
+    for copy in mv_loads:
+        copy.start()
 
     group = max(g for g in range(1, 33) if chunk % g == 0)
 
@@ -115,8 +120,13 @@
     lane = lax.broadcasted_iota(jnp.int32, (rows, 128), 1)
     shift_l = off % 128
     shift_r = off // 128
-    for j, ref in enumerate((m_ref, v_ref)):
-        x = pltpu.roll(ref[...], shift_l, 1)
+    whole = step * TILE
+    for j, ref in enumerate((m_in, v_in)):
+        mv_loads[j].wait()
+        edge = jnp.pad(ref[pl.ds(whole, shard - whole)], (0, 128 - (shard - whole)))
+        edge = jnp.broadcast_to(edge.reshape(1, 128), (8, 128))
+        x = jnp.concatenate([ref[pl.ds(0, whole)].reshape(step * 8, 128), edge], 0)
+        x = pltpu.roll(x, shift_l, 1)
         x = jnp.where(lane < shift_l, pltpu.roll(x, 1, 0), x)
         x = pltpu.roll(x, shift_r, 0)
         mv[:, j] = x.reshape(span, 8, 128)
@@ -266,11 +276,6 @@
     def same(index, core):
         return (index // n_spa) * (2 * n_spa) + core * n_spa + index % n_spa
 
-    def put(block):
-        return pltpu.make_async_copy(
-            ags.at[block, pl.ds(0, step)], out_ref.at[pl.ds(block * step, step)], out_sem.at[block]
-        )
-
     def to_plane(zz):
         block = zz * plane + p
 
@@ -282,7 +287,6 @@
     def to_partner(zz, index):
         block = zz * plane + same(index, c)
         copy4(block, n_out + n_out * n_same + zz * n_same + index, partner).start()
-        put(block).start()
 
     @pl.loop(1, n_out)
     def _(k):
@@ -291,13 +295,6 @@
 
     to_plane(z)
     to_partner(z, me_same)
-
-    back_l = 128 - shift_l
-    for ref, src in ((nm_ref, nmw), (nv_ref, nvw)):
-        x = src[...].reshape(rows, 128)
-        x = pltpu.roll(x, (rows - shift_r) % rows, 0)
-        x = pltpu.roll(x, back_l % 128, 1)
-        ref[...] = jnp.where(lane < back_l, x, pltpu.roll(x, rows - 1, 0))
 
     @pl.loop(1, n_out)
     def _(k):
@@ -325,14 +322,6 @@
             peer = (me_same + q) % n_same
             block = zz * plane + same(peer, 1 - c)
             copy4(block, 0, d).wait_recv()
-            put(block).start()
-
-    tail = pltpu.make_async_copy(
-        ags.at[n - 1, pl.ds(step, span - step)],
-        out_ref.at[pl.ds(n * step, span - step)],
-        out_sem.at[n],
-    )
-    tail.start()
 
     @pl.loop(1, n_out)
     def _(k):
@@ -360,11 +349,44 @@
     def _(q):
         copy3(d, (d + q) % n).wait_send()
 
-    @pl.loop(0, n)
-    def _(block):
-        put(block).wait()
-
-    tail.wait()
+
+def finish(plan, ags, nmw, nvw, out_ref, nm_ref, nv_ref, nm_out, nv_out, out_sem, own_sem):
+    n, n_spa, shard, step, span = plan
+    rows = span * 8
+    whole = step * TILE
+    copies = [
+        pltpu.make_async_copy(
+            ags.at[b, pl.ds(0, step)], out_ref.at[pl.ds(b * step, step)], out_sem.at[b]
+        )
+        for b in range(n)
+    ]
+    copies.append(
+        pltpu.make_async_copy(
+            ags.at[n - 1, pl.ds(step, span - step)],
+            out_ref.at[pl.ds(n * step, span - step)],
+            out_sem.at[n],
+        )
+    )
+    for copy in copies:
+        copy.start()
+    d = lax.axis_index("replica") * n_spa + lax.axis_index("spatial")
+    off = d * (shard - whole)
+    shift_l = off % 128
+    shift_r = off // 128
+    back_l = 128 - shift_l
+    lane = lax.broadcasted_iota(jnp.int32, (rows, 128), 1)
+    for j, (src, buf, ref) in enumerate(((nmw, nm_out, nm_ref), (nvw, nv_out, nv_ref))):
+        x = src[...].reshape(rows, 128)
+        x = pltpu.roll(x, (rows - shift_r) % rows, 0)
+        x = pltpu.roll(x, back_l % 128, 1)
+        x = jnp.where(lane < back_l, x, pltpu.roll(x, rows - 1, 0))
+        buf[pl.ds(0, whole)] = x[: step * 8].reshape(whole)
+        buf[pl.ds(whole, shard - whole)] = x[step * 8, : shard - whole].reshape(shard - whole)
+        copy = pltpu.make_async_copy(buf, ref, own_sem.at[j])
+        copy.start()
+        copies.append(copy)
+    for copy in copies:
+        copy.wait()
 
 
 def windowed(n_rep, n_spa, grads, master, velocity, layer_offsets, layer_sizes, lars_skip):
@@ -379,25 +401,25 @@
     span = params // TILE - (n - 1) * step
     chunk = (plane - 1) * step + span
     tiles = params // TILE
-    rows = span * 8
-    pad = span * TILE - shard
     plan = (n_out, n_a, n_spa, shard, step, span, layers)
     vmem = pl.BlockSpec(memory_space=pltpu.VMEM)
     smem = pl.BlockSpec(memory_space=pltpu.SMEM)
-    anywhere = pl.BlockSpec(memory_space=pl.ANY)
+    anywhere = pl.BlockSpec(memory_space=pltpu.HBM)
     f32, bf16 = jnp.float32, jnp.bfloat16
     dma = pltpu.SemaphoreType.DMA
     n_same = plane // 2
-    weights, nm, nv = pl.pallas_call(
+    ags, nmw, nvw = pl.pallas_call(
         functools.partial(kernel, plan),
         out_shape=(
-            jax.ShapeDtypeStruct((tiles, 8, 128), bf16),
-            jax.ShapeDtypeStruct((rows, 128), f32),
-            jax.ShapeDtypeStruct((rows, 128), f32),
+            pltpu.VMEM((n, span, 8, 128), bf16),
+            pltpu.VMEM((span, 8, 128), f32),
+            pltpu.VMEM((span, 8, 128), f32),
         ),
-        in_specs=[anywhere, vmem, vmem, smem, smem, smem],
-        out_specs=(anywhere, vmem, vmem),
+        in_specs=[anywhere, anywhere, anywhere, smem, smem, smem],
+        out_specs=(vmem, vmem, vmem),
         scratch_shapes=[
+            pltpu.VMEM((shard,), f32),
+            pltpu.VMEM((shard,), f32),
             pltpu.VMEM((n_out, 1, chunk * TILE), bf16),
             pltpu.VMEM((n_out, chunk, 8, 128), bf16),
             pltpu.VMEM((n_out, plane, span, 8, 128), bf16),
@@ -408,10 +430,8 @@
             pltpu.VMEM((span, 8, 128), f32),
             pltpu.VMEM((1, 128), f32),
             pltpu.VMEM((n, 1, 128), f32),
-            pltpu.VMEM((n, span, 8, 128), bf16),
-            pltpu.VMEM((span, 8, 128), f32),
-            pltpu.VMEM((span, 8, 128), f32),
             dma((n_out,)),
+            dma((2,)),
             dma((n_out, plane)),
             dma((n_out, plane)),
             dma((n_out,)),
@@ -421,18 +441,29 @@
             dma((n,)),
             dma((n_out + 2 * n_out * n_same,)),
             dma((n,)),
+        ],
+        compiler_params=pltpu.CompilerParams(
+            collective_id=0, has_side_effects=True, vmem_limit_bytes=61 * 2**20
+        ),
+    )(grads, master, velocity, layer_offsets, layer_sizes, lars_skip)
+    weights, nm, nv = pl.pallas_call(
+        functools.partial(finish, (n, n_spa, shard, step, span)),
+        out_shape=(
+            jax.ShapeDtypeStruct((tiles, 8, 128), bf16),
+            jax.ShapeDtypeStruct((shard,), f32),
+            jax.ShapeDtypeStruct((shard,), f32),
+        ),
+        in_specs=[vmem, vmem, vmem],
+        out_specs=(anywhere, anywhere, anywhere),
+        scratch_shapes=[
+            pltpu.VMEM((shard,), f32),
+            pltpu.VMEM((shard,), f32),
             dma((n + 1,)),
+            dma((2,)),
         ],
-        compiler_params=pltpu.CompilerParams(collective_id=0, has_side_effects=True),
-    )(
-        grads,
-        jnp.pad(master, (0, pad)).reshape(rows, 128),
-        jnp.pad(velocity, (0, pad)).reshape(rows, 128),
-        layer_offsets,
-        layer_sizes,
-        lars_skip,
-    )
-    return weights.reshape(params), nm.reshape(-1)[:shard], nv.reshape(-1)[:shard]
+        compiler_params=pltpu.CompilerParams(vmem_limit_bytes=16 * 2**20),
+    )(ags, nmw, nvw)
+    return weights.reshape(params), nm, nv
 
 
 def tiled(n_rep, n_spa, params):
@@ -446,6 +477,7 @@
         and params % TILE == 0
         and shard >= TILE
         and 0 < n * rest <= TILE
+        and rest <= 128
     )
 
 

time: 60.9 us -> 55.2 us (0.906)
  the two profiles are of different devices: /device:TPU:0 before, /device:TPU:9 now
where the time goes in v2:
time: 55.2 us; the launch traced here: 55 us
  Pallas kernels  54.4 us (99%)
  between operations  0.64 us (1%)
    pallas_call x1, Pallas kernels, windowed(): pl.pallas_call(functools.partial(kernel, plan), out_shape=(pltpu.VMEM((n,...  52.8 us
    pallas_call x1, Pallas kernels, windowed(): pl.pallas_call(functools.partial(finish, (n, n_spa, shard, step, span)),...  1.57 us

profile of v2, /device:TPU:9, one launch (start us, length us, event | category | flops | bytes accessed | tf_op | source)
XLA Modules:
  0.0 55.0 jit_solution(2905659574148180479)
XLA Ops:
  0.6 52.8 %shard_map.85 = (bf16[32,27,8,128]{3,2,1,0:T(8,128)(2,1)S(1)}, f32[27,8,128]{2,1,0:T(8,128)S(1)}, f32[27,8,128]{2,1,0:T(8,128)S(1)}) custom-call(bf16[1,1,852992]{2,1,0:T(2,128)(2,1)} %grads_ref.1, f32[26656]{0:T(1024)} %m_ref.1, f32[26656]{0:T(1024)} %v_ref.1, s32[6]{0:T(128)} %offsets_ref.1, s32[6]{0:T(128)} %sizes_ref.1, s32[6]{0:T(128)} %skip_ref.1), custom_call_target="tpu_custom_call" | custom-call | tf_op jit(solution)/shard_map/pallas_call | solution.py:411
  53.4 1.6 %shard_map.86 = (bf16[833,8,128]{2,1,0:T(8,128)(2,1)}, f32[26656]{0:T(1024)}, f32[26656]{0:T(1024)}) custom-call(bf16[32,27,8,128]{3,2,1,0:T(8,128)(2,1)S(1)} %get-tuple-element.9.ags, f32[27,8,128]{2,1,0:T(8,128)S(1)} %get-tuple-element.10.nmw, f32[27,8,128]{2,1,0:T(8,128)S(1)} %get-tuple-element.11.nvw), custom_call_target="tpu_custom_call" | custom-call | tf_op jit(solution)/shard_map/pallas_call | solution.py:449

commit v3 on v2

--- a/solution.py
+++ b/solution.py
@@ -67,10 +67,6 @@
 
     barrier = pltpu.get_barrier_semaphore()
 
-    @pl.loop(1, n)
-    def _(q):
-        pl.semaphore_signal(barrier, inc=1, device_id=dev((d + q) % n), device_id_type=MESH)
-
     def load(zt):
         start = pl.multiple_of(zt * (plane * step * TILE), TILE)
         return pltpu.make_async_copy(
@@ -86,6 +82,10 @@
     for copy in mv_loads:
         copy.start()
 
+    @pl.loop(1, n, unroll=True)
+    def _(q):
+        pl.semaphore_signal(barrier, inc=1, device_id=dev((d + q) % n), device_id_type=MESH)
+
     group = max(g for g in range(1, 33) if chunk % g == 0)
 
     def pack(zt):
@@ -101,7 +101,7 @@
         return pltpu.make_async_remote_copy(
             src_ref=packed.at[zt, pl.ds(dst * step, span)],
             dst_ref=recv1.at[zt, src],
-            send_sem=send1.at[zt, dst],
+            send_sem=send1,
             recv_sem=got1.at[zt, src],
             device_id=dev(z * plane + dst),
             device_id_type=MESH,
@@ -113,7 +113,7 @@
         if k == 1:
             pl.semaphore_wait(barrier, n - 1)
 
-        @pl.loop(1, plane)
+        @pl.loop(1, plane, unroll=True)
         def _(q):
             copy1(zt, p, (p + q) % plane).start()
 
@@ -173,7 +173,7 @@
         return pltpu.make_async_remote_copy(
             src_ref=part.at[zt],
             dst_ref=recv2.at[src],
-            send_sem=send2.at[zt],
+            send_sem=send2,
             recv_sem=got2.at[src],
             device_id=dev(zt * plane + p),
             device_id_type=MESH,
@@ -217,17 +217,17 @@
         return pltpu.make_async_remote_copy(
             src_ref=stats.at[src],
             dst_ref=stats.at[src],
-            send_sem=send3.at[dst],
+            send_sem=send3,
             recv_sem=got3.at[src],
             device_id=dev(dst),
             device_id_type=MESH,
         )
 
-    @pl.loop(1, n)
+    @pl.loop(1, n, unroll=True)
     def _(q):
         copy3(d, (d + q) % n).start()
 
-    @pl.loop(1, n)
+    @pl.loop(1, n, unroll=True)
     def _(q):
         copy3((d + q) % n, d).wait_recv()
 
@@ -259,11 +259,11 @@
         nmw[t] = nm
         ags[d, t] = nm.astype(jnp.bfloat16)
 
-    def copy4(block, slot, dst):
+    def copy4(block, dst):
         return pltpu.make_async_remote_copy(
             src_ref=ags.at[block],
             dst_ref=ags.at[block],
-            send_sem=send4.at[slot],
+            send_sem=send4,
             recv_sem=got4.at[block],
             device_id=dev(dst),
             device_id_type=MESH,
@@ -282,16 +282,16 @@
         @pl.loop(1, n_same)
         def _(q):
             peer = (me_same + q) % n_same
-            copy4(block, n_out + zz * n_same + peer, z * plane + same(peer, c)).start()
+            copy4(block, z * plane + same(peer, c)).start()
 
     def to_partner(zz, index):
         block = zz * plane + same(index, c)
-        copy4(block, n_out + n_out * n_same + zz * n_same + index, partner).start()
+        copy4(block, partner).start()
 
     @pl.loop(1, n_out)
     def _(k):
         zz = (z + k) % n_out
-        copy4(d, zz, zz * plane + p).start()
+        copy4(d, zz * plane + p).start()
 
     to_plane(z)
     to_partner(z, me_same)
@@ -299,7 +299,7 @@
     @pl.loop(1, n_out)
     def _(k):
         zz = (z + k) % n_out
-        copy4(zz * plane + p, zz, d).wait_recv()
+        copy4(zz * plane + p, d).wait_recv()
         to_plane(zz)
         to_partner(zz, me_same)
 
@@ -310,7 +310,7 @@
         @pl.loop(1, n_same)
         def _(q):
             peer = (me_same + q) % n_same
-            copy4(zz * plane + same(peer, c), 0, d).wait_recv()
+            copy4(zz * plane + same(peer, c), d).wait_recv()
             to_partner(zz, peer)
 
     @pl.loop(0, n_out)
@@ -321,33 +321,15 @@
         def _(q):
             peer = (me_same + q) % n_same
             block = zz * plane + same(peer, 1 - c)
-            copy4(block, 0, d).wait_recv()
-
-    @pl.loop(1, n_out)
-    def _(k):
-        zz = (z + k) % n_out
-        copy2(zz, z).wait_send()
-        copy4(d, zz, zz * plane + p).wait_send()
-
-    @pl.loop(0, n_out)
-    def _(zz):
-        @pl.loop(1, plane)
-        def _(q):
-            copy1(zz, p, (p + q) % plane).wait_send()
-
-        @pl.loop(1, n_same)
-        def _(q):
-            peer = (me_same + q) % n_same
-            copy4(zz * plane + p, n_out + zz * n_same + peer, z * plane + same(peer, c)).wait_send()
-
-        @pl.loop(0, n_same)
-        def _(index):
-            slot = n_out + n_out * n_same + zz * n_same + index
-            copy4(zz * plane + same(index, c), slot, partner).wait_send()
-
-    @pl.loop(1, n)
-    def _(q):
-        copy3(d, (d + q) % n).wait_send()
+            copy4(block, d).wait_recv()
+
+    for ref, sem in (
+        (recv1.at[:, pl.ds(0, plane - 1)], send1),
+        (recv2.at[pl.ds(0, n_out - 1)], send2),
+        (stats.at[pl.ds(0, n - 1)], send3),
+        (ags.at[pl.ds(0, n - 1)], send4),
+    ):
+        pltpu.make_async_copy(ref, ref, sem).wait()
 
 
 def finish(plan, ags, nmw, nvw, out_ref, nm_ref, nv_ref, nm_out, nv_out, out_sem, own_sem):
@@ -407,7 +389,6 @@
     anywhere = pl.BlockSpec(memory_space=pltpu.HBM)
     f32, bf16 = jnp.float32, jnp.bfloat16
     dma = pltpu.SemaphoreType.DMA
-    n_same = plane // 2
     ags, nmw, nvw = pl.pallas_call(
         functools.partial(kernel, plan),
         out_shape=(
@@ -432,14 +413,14 @@
             pltpu.VMEM((n, 1, 128), f32),
             dma((n_out,)),
             dma((2,)),
+            dma(()),
             dma((n_out, plane)),
-            dma((n_out, plane)),
-            dma((n_out,)),
+            dma(()),
             dma((n_out,)),
             dma((2,)),
+            dma(()),
             dma((n,)),
-            dma((n,)),
-            dma((n_out + 2 * n_out * n_same,)),
+            dma(()),
             dma((n,)),
         ],
         compiler_params=pltpu.CompilerParams(

time: 55.2 us -> 53 us (0.960)
  the two profiles are of different devices: /device:TPU:9 before, /device:TPU:0 now
where the time goes in v3:
time: 53 us; the launch traced here: 52.8 us
  Pallas kernels  52.2 us (98%)
  between operations  0.64 us (1%)
    pallas_call x1, Pallas kernels, windowed(): pl.pallas_call(functools.partial(kernel, plan), out_shape=(pltpu.VMEM((n,...  50.6 us
    pallas_call x1, Pallas kernels, windowed(): pl.pallas_call(functools.partial(finish, (n, n_spa, shard, step, span)),...  1.57 us

profile of v3, /device:TPU:0, one launch (start us, length us, event | category | flops | bytes accessed | tf_op | source)
XLA Modules:
  0.0 52.8 jit_solution(9287251010495428475)
XLA Ops:
  0.6 50.6 %shard_map.85 = (bf16[32,27,8,128]{3,2,1,0:T(8,128)(2,1)S(1)}, f32[27,8,128]{2,1,0:T(8,128)S(1)}, f32[27,8,128]{2,1,0:T(8,128)S(1)}) custom-call(bf16[1,1,852992]{2,1,0:T(2,128)(2,1)} %grads_ref.1, f32[26656]{0:T(1024)} %m_ref.1, f32[26656]{0:T(1024)} %v_ref.1, s32[6]{0:T(128)} %offsets_ref.1, s32[6]{0:T(128)} %sizes_ref.1, s32[6]{0:T(128)} %skip_ref.1), custom_call_target="tpu_custom_call" | custom-call | tf_op jit(solution)/shard_map/pallas_call | solution.py:392
  51.2 1.6 %shard_map.86 = (bf16[833,8,128]{2,1,0:T(8,128)(2,1)}, f32[26656]{0:T(1024)}, f32[26656]{0:T(1024)}) custom-call(bf16[32,27,8,128]{3,2,1,0:T(8,128)(2,1)S(1)} %get-tuple-element.9.ags, f32[27,8,128]{2,1,0:T(8,128)S(1)} %get-tuple-element.10.nmw, f32[27,8,128]{2,1,0:T(8,128)S(1)} %get-tuple-element.11.nvw), custom_call_target="tpu_custom_call" | custom-call | tf_op jit(solution)/shard_map/pallas_call | solution.py:430
